TPU v7x, 128 devices: a whole 4x4x4 slice. The times are simulated.
128 devices in a mesh: fsdp: 16 (over z, x_lo, core), cols: 8 (over y, x_hi).
Axes of the slice: x: 4 (x_hi: 2, x_lo: 2; x = x_hi * 2 + x_lo), y: 4, z: 4, core: 2. Of those that a mesh axis runs over, the one named last changes fastest.
Arguments:
- weight_query: bfloat16 [5120, 5120], P('fsdp', 'cols'), may hold values from -0.078125 to 0.078125
- low_query: bfloat16 [5120, 32], P('fsdp'), may hold values from -0.078125 to 0.078125
- high_query: bfloat16 [32, 5120], P(None, 'cols'), may hold values from -1 to 1
- weight_key: bfloat16 [5120, 5120], P('fsdp', 'cols'), may hold values from -0.078125 to 0.078125
- low_key: bfloat16 [5120, 32], P('fsdp'), may hold values from -0.078125 to 0.078125
- high_key: bfloat16 [32, 5120], P(None, 'cols'), may hold values from -1 to 1
- weight_value: bfloat16 [5120, 5120], P('fsdp', 'cols'), may hold values from -0.078125 to 0.078125
- low_value: bfloat16 [5120, 32], P('fsdp'), may hold values from -0.078125 to 0.078125
- high_value: bfloat16 [32, 5120], P(None, 'cols'), may hold values from -1 to 1
- weight_mixed: bfloat16 [5120, 5120], P('cols', 'fsdp'), may hold values from -0.078125 to 0.078125
- low_mixed: bfloat16 [5120, 32], P('cols'), may hold values from -0.078125 to 0.078125
- high_mixed: bfloat16 [32, 5120], P(None, 'fsdp'), may hold values from -1 to 1
- norm_train: float32 [5120], P(('fsdp', 'cols')), may hold values from 0.25 to 1.75
- norm_step: float32 [5120], P(('fsdp', 'cols')), may hold values from -0.3 to 0.3
Outputs:
- ready_query: bfloat16 [5120, 5120], P(None, 'cols')
- ready_key: bfloat16 [5120, 5120], P(None, 'cols')
- ready_value: bfloat16 [5120, 5120], P(None, 'cols')
- ready_mixed: bfloat16 [5120, 5120], P('cols')
- serve_norm: bfloat16 [5120], replicated
All inputs are finite; a program needn't handle non-finite values.
Results may differ from a plain program's by a relative error of at most 0.001.
Values may be sent and summed in bfloat16 or wider, within the bound.
A program may use at most 192 MiB of HBM per device.

v0:
```python
import jax
import jax.numpy as jnp
from jax import lax
from jax.sharding import PartitionSpec as P

mix_rate = 2.0


def rows_first(arrays, axis, dims):
    turned = [jnp.moveaxis(a, dim, 0) for a, dim in zip(arrays, dims)]
    widths = [t[0].size for t in turned]
    both = jnp.concatenate([t.reshape(-1, w) for t, w in zip(turned, widths)], axis=1)
    result = lax.all_gather(both, axis, axis=0, tiled=True)
    blocks = jnp.split(result, [sum(widths[:k]) for k in range(1, len(widths))], axis=1)
    return tuple(
        (
            jnp.moveaxis(b.reshape(-1, *t.shape[1:]), 0, dim)
            for b, t, dim in zip(blocks, turned, dims)
        )
    )


def per_device(
    weight_query,
    low_query,
    high_query,
    weight_key,
    low_key,
    high_key,
    weight_value,
    low_value,
    high_value,
    weight_mixed,
    low_mixed,
    high_mixed,
    norm_train,
    norm_step,
):
    latest_query = weight_query.astype(jnp.float32) + mix_rate * jnp.dot(
        low_query, high_query, preferred_element_type=jnp.float32
    )
    latest_key = weight_key.astype(jnp.float32) + mix_rate * jnp.dot(
        low_key, high_key, preferred_element_type=jnp.float32
    )
    latest_value = weight_value.astype(jnp.float32) + mix_rate * jnp.dot(
        low_value, high_value, preferred_element_type=jnp.float32
    )
    latest_mixed = weight_mixed.astype(jnp.float32) + mix_rate * jnp.dot(
        low_mixed, high_mixed, preferred_element_type=jnp.float32
    )
    narrow_query, narrow_key, narrow_value, narrow_mixed = (
        latest_query.astype(jnp.bfloat16),
        latest_key.astype(jnp.bfloat16),
        latest_value.astype(jnp.bfloat16),
        latest_mixed.astype(jnp.bfloat16),
    )
    ready_query, ready_key, ready_value, ready_mixed = rows_first(
        (narrow_query, narrow_key, narrow_value, narrow_mixed), "fsdp", (0, 0, 0, 1)
    )
    serve_norm = lax.all_gather(
        (norm_train + norm_step).astype(jnp.bfloat16), ("fsdp", "cols"), axis=0, tiled=True
    )
    return (ready_query, ready_key, ready_value, ready_mixed, serve_norm)


def solution(mesh):
    in_specs = (
        P("fsdp", "cols"),
        P("fsdp", None),
        P(None, "cols"),
        P("fsdp", "cols"),
        P("fsdp", None),
        P(None, "cols"),
        P("fsdp", "cols"),
        P("fsdp", None),
        P(None, "cols"),
        P("cols", "fsdp"),
        P("cols", None),
        P(None, "fsdp"),
        P(("fsdp", "cols")),
        P(("fsdp", "cols")),
    )
    out_specs = (P(None, "cols"), P(None, "cols"), P(None, "cols"), P("cols", None), P())
    return jax.shard_map(
        per_device, mesh=mesh, in_specs=in_specs, out_specs=out_specs, check_vma=False
    )
```

profile of v0, /device:TPU:1, one launch (start us, length us, event | category | flops | bytes accessed | tf_op | source)
XLA Modules:
  0.0 190.2 jit_solution(9804116227767435953)
XLA Ops:
  7.2 0.0 copy-start
  7.2 0.0 all-gather.2.cloned.1.call-start
  7.2 0.7 copy-done
  8.0 1.3 fusion.4
  9.3 1.3 fusion.5
  10.6 0.0 copy-start.1
  10.6 0.0 copy-start.2
  10.6 1.3 fusion.6
  12.0 1.4 fusion.8
  13.4 1.3 pad_maximum_fusion
  14.7 0.0 all-gather.2.cloned.1.call-update
  14.7 0.0 copy-done.1
  14.7 0.0 copy-done.2
  14.7 0.2 dynamic-update-slice
  15.0 68.9 %all-reduce = bf16[5120]{0:T(1024)(128)(2,1)} all-reduce(bf16[5120]{0:T(1024)(128)(2,1)S(1)} %dynamic-update-slice), channel_id=1, replica_groups=mesh['fsdp'=16,'cols'=8] {'fsdp','cols'}, use_global_device_ids=true, to_apply=%add | all-reduce | flops 5120 | bytes 20480
  83.9 71.9 %all-gather.2.cloned.1.call-done = bf16[5120,2560]{1,0:T(8,128)(2,1)} async-done(((bf16[320,2560]{1,0:T(8,128)(2,1)}), bf16[5120,2560]{1,0:T(8,128)(2,1)}) %all-gather.2.cloned.1.call-update) | async-done | bytes 26214416 | tf_op jit(solution)/shard_map/all_gather | solution.py:13
  155.7 18.1 %slice_bitcast_fusion = (bf16[640,5120]{0,1:T(8,128)(2,1)}, bf16[5120,640]{1,0:T(8,128)(2,1)}, bf16[5120,640]{1,0:T(8,128)(2,1)}, bf16[5120,640]{1,0:T(8,128)(2,1)}) fusion(bf16[5120,2560]{1,0:T(8,128)(2,1)} %all-gather.2.cloned.1.call-done), kind=kLoop, calls=%fused_computation | loop fusion | bytes 52428800 | tf_op jit(solution)/shard_map/transpose | solution.py:17
  173.8 9.5 %copy.19 = bf16[640,5120]{1,0:T(8,128)(2,1)} copy(bf16[640,5120]{0,1:T(8,128)(2,1)} %get-tuple-element.10) | data formatting | bytes 13107200
  (2 shorter events, 0.0 us)
Async XLA Ops:
  7.2 0.8 copy-start
  7.2 148.5 %all-gather.2.cloned.1.call-start = ((), (), s32[]{:S(2)}) async-start(), calls=%async_computation | async-start | bytes 27852800 | tf_op jit(solution)/shard_map/all_gather | solution.py:13
  10.6 4.1 %copy-start.1 = (f32[40]{0:T(128)S(1)}, f32[40]{0:T(128)}, u32[]{:S(2)}) copy-start(f32[40]{0:T(128)} %param.26) | copy-start | bytes 484
  10.6 4.1 %copy-start.2 = (f32[40]{0:T(128)S(1)}, f32[40]{0:T(128)}, u32[]{:S(2)}) copy-start(f32[40]{0:T(128)} %param.27) | copy-start | bytes 484
Sparse Core Ops, SparseCore 0:
  14.8 140.8 all-gather.1
where the time goes:
time: 191 us; the launch traced here: 190 us
  waiting for transfers between devices  71.9 us (38%)
  blocking collectives  68.9 us (36%)
  local copies, waits for them, and re-layouts  28.6 us (15%)
  between operations  14.1 us (7%)
  matrix products  5.36 us (3%)
    all_gather x1, waiting for transfers between devices, rows_first(): result = lax.all_gather(both, axis, axis=0, tiled=True)  71.9 us
    unnamed x1, blocking collectives  68.9 us
    transpose x1, local copies, waits for them, and re-layouts, rows_first(): jnp.moveaxis(b.reshape(-1, *t.shape[1:]), 0, dim)  18.1 us
    unnamed x9, local copies, waits for them, and re-layouts  10.5 us
  transfers between devices with their start and end apart: 1, of which 1 were waited for; matrix products, arithmetic and copies ran while one was open for 0% of the time, Pallas kernels for 0%

commit v1 on v0

v1 whole, which is shorter than its diff:
```python
import functools
import heapq

import jax
import jax.numpy as jnp
from jax import lax
from jax.experimental import pallas as pl
from jax.experimental.pallas import tpu as pltpu
from jax.sharding import PartitionSpec as P

mix_rate = 2.0

Z, X, CORES = 4, 2, 2
CHIPS = Z * X
ROWS, WIDTH, RANK = 320, 640, 32
FULL = ROWS * CHIPS * CORES
RING_FIRST, ACROSS_FIRST = 0, 1
PART = ((0, 144), (144, 176))
RIGHT, LEFT, ACROSS = 0, 1, 2
LINKS = (RIGHT, LEFT, ACROSS)


def onward(dz, dx, array, part, via):
    links = []
    if part == RING_FIRST and dx == 0:
        links.append(ACROSS)
    if part == ACROSS_FIRST and (dz, dx) == (0, 1):
        links += [RIGHT, LEFT]
    if via == RIGHT and dz == 3 and array < 2:
        links.append(RIGHT)
    if via == LEFT and dz == 1 and array >= 2:
        links.append(LEFT)
    return links


def seen_by_receiver(dz, dx, link):
    if link == RIGHT:
        return (dz - 1) % Z, dx
    if link == LEFT:
        return (dz + 1) % Z, dx
    return dz, 1 - dx


def first_sends():
    early, late = [], []
    for array in range(4):
        into = early if array < 3 else late
        into += [(ACROSS, array, ACROSS_FIRST), (RIGHT, array, RING_FIRST), (LEFT, array, RING_FIRST)]
    for array in range(4):
        late += [(ACROSS, array, RING_FIRST), (RIGHT, array, ACROSS_FIRST), (LEFT, array, ACROSS_FIRST)]
    return early, late


def arrivals():
    rate, latency = 46.7e3, 2.0
    free = [0.0] * 3
    queue, order = [], []

    def send(now, link, unit):
        took = PART[unit[3]][1] * WIDTH * 2 / rate
        free[link] = max(free[link], now) + took
        heapq.heappush(queue, (free[link] + latency, len(queue) + 1000 * len(order), link, unit))

    early, late = first_sends()
    for link, array, part in early + late:
        send(0.0, link, (0, 0, array, part))
    while queue:
        now, _, via, (dz, dx, array, part) = heapq.heappop(queue)
        dz, dx = seen_by_receiver(dz, dx, via)
        order.append((dz, dx, array, part, via))
        for link in onward(dz, dx, array, part, via):
            send(now, link, (dz, dx, array, part))
    return order


def merge(weight, left, right):
    product = lax.dot_general(left, right, (((0,), (0,)), ((), ())), preferred_element_type=jnp.float32)
    return (weight.astype(jnp.float32) + mix_rate * product).astype(jnp.bfloat16)


def gather_kernel(
    cols,
    weight_query, low_query, high_query,
    weight_key, low_key, high_key,
    weight_value, low_value, high_value,
    weight_mixed, low_mixed, high_mixed,
    norm_train, norm_step,
    full_query, full_key, full_value, full_mixed, norm_slots,
    weights, lefts, rights, mixed_pair, norms, norm_parts,
    in_sem, link_send, link_recv, core_send, core_recv, pair_sem, norm_send, near_recv, far_recv,
):
    f, c = lax.axis_index("fsdp"), lax.axis_index("cols")
    z, x, core = lax.div(f, X * CORES), lax.rem(lax.div(f, CORES), X), lax.rem(f, CORES)
    chip = lax.div(f, CORES)
    fulls = (full_query, full_key, full_value, full_mixed)

    def at(device_z, device_x, device_core):
        return device_z * (X * CORES) + device_x * CORES + device_core

    neighbour = {
        RIGHT: at(lax.rem(z + 1, Z), x, core),
        LEFT: at(lax.rem(z + Z - 1, Z), x, core),
        ACROSS: at(z, 1 - x, core),
    }
    twin = at(z, x, 1 - core)

    loads = []

    def load(source, target):
        copy = pltpu.make_async_copy(source, target, in_sem.at[len(loads)])
        copy.start()
        loads.append(copy)

    inputs = (
        (weight_query, low_query, high_query),
        (weight_key, low_key, high_key),
        (weight_value, low_value, high_value),
        (weight_mixed, high_mixed, low_mixed),
    )
    for k, (weight, left, right) in enumerate(inputs):
        load(weight, weights.at[k])
        load(left, lefts.at[k])
        load(right, rights.at[k])
    load(norm_train, norms.at[0])
    load(norm_step, norms.at[1])

    near = [(dc, dk) for dc in range(cols) for dk in range(CORES) if (dc, dk) != (0, 0)]
    far = [(dz, dx) for dz in range(Z) for dx in range(X) if (dz, dx) != (0, 0)]

    def near_id(dc, dk):
        return {"fsdp": at(z, x, lax.rem(core + dk, CORES)), "cols": lax.rem(c + dc, cols)}

    def far_id(dz, dx):
        return {"fsdp": at(lax.rem(z + dz, Z), lax.rem(x + dx, X), core)}

    barrier = pltpu.get_barrier_semaphore()
    for peer in [near_id(*d) for d in near] + [far_id(*d) for d in far]:
        pl.semaphore_signal(barrier, inc=1, device_id=peer, device_id_type=pl.DeviceIdType.MESH)

    def wait_loads(k):
        for copy in loads[3 * k : 3 * k + 3]:
            copy.wait()

    own_rows = pl.ds(pl.multiple_of(f * ROWS, 16), ROWS)
    wait_loads(3)
    own_half = pl.ds(pl.multiple_of(core * ROWS, 16), ROWS)
    mixed_pair[own_half, :] = merge(weights[3], lefts[3], rights[3])
    for k in range(3):
        wait_loads(k)
        fulls[k][own_rows, :] = merge(weights[k], lefts[k], rights[k])
    pl.semaphore_wait(barrier, len(near) + len(far))

    sends = []

    def remote(source, target, send_sem, recv_sem, device):
        copy = pltpu.make_async_remote_copy(
            src_ref=source,
            dst_ref=target,
            send_sem=send_sem,
            recv_sem=recv_sem,
            device_id=device if isinstance(device, dict) else {"fsdp": device},
            device_id_type=pl.DeviceIdType.MESH,
        )
        copy.start()
        sends.append(copy)

    def view(dz, dx, device_core, array, start, rows):
        block = lax.rem(z + dz, Z) * X + lax.rem(x + dx, X)
        if array < 3:
            first = (block * CORES + device_core) * ROWS + start
            return fulls[array].at[pl.ds(pl.multiple_of(first, 16), rows), :]
        first = device_core * ROWS + start
        return full_mixed.at[
            pl.ds(pl.multiple_of(first, 16), rows), pl.ds(pl.multiple_of(block * WIDTH, 128), WIDTH)
        ]

    def place(dz, dx, array, part):
        return ((dz * X + dx) * 4 + array) * 2 + part

    counts = {"link": 0, "core": 0}

    def send_on(link, dz, dx, array, part):
        block = view(dz, dx, core, array, *PART[part])
        there = place(*seen_by_receiver(dz, dx, link), array, part)
        remote(block, block, link_send.at[counts["link"]], link_recv.at[there], neighbour[link])
        counts["link"] += 1

    def hand_over(dz, dx, array, part):
        block = view(dz, dx, core, array, *PART[part])
        remote(block, block, core_send.at[counts["core"]], core_recv.at[place(dz, dx, array, part)], twin)
        counts["core"] += 1

    early, late = first_sends()
    half = mixed_pair.at[own_half, :]
    remote(half, half, pair_sem.at[0], pair_sem.at[1], twin)
    pair = sends[-1]
    for link, array, part in early:
        send_on(link, 0, 0, array, part)
    for array in range(3):
        for part in (RING_FIRST, ACROSS_FIRST):
            hand_over(0, 0, array, part)

    for copy in loads[12:]:
        copy.wait()
    piece = norms.shape[-1]
    gain = (norms[0] + norms[1]).astype(jnp.bfloat16)
    gain = jnp.broadcast_to(gain.astype(jnp.float32), (8, piece)).astype(jnp.bfloat16)
    offset = (core * cols + c) * piece
    lane = lax.broadcasted_iota(jnp.int32, (piece, 128), 1)
    element = lax.broadcasted_iota(jnp.int32, (piece, 128), 0)
    row = lax.broadcasted_iota(jnp.int32, (8, 128), 0)
    tile = jnp.zeros((8, 128), jnp.float32)
    for r in range(5):
        hot = jnp.where(lane + 128 * r == element + offset, 1.0, 0.0).astype(jnp.bfloat16)
        spread = jnp.dot(gain, hot, preferred_element_type=jnp.float32)
        tile = jnp.where(row == r, spread, tile)
    norm_parts[0] = tile

    pair.wait_recv()
    turned = mixed_pair[...].astype(jnp.float32).T.astype(jnp.bfloat16)
    full_mixed[:, pl.ds(pl.multiple_of(chip * WIDTH, 128), WIDTH)] = turned

    for n, (dc, dk) in enumerate(near):
        slot = ((cols - dc) % cols) * CORES + dk
        remote(norm_parts.at[0], norm_parts.at[slot], norm_send.at[n], near_recv.at[slot], near_id(dc, dk))

    for link, array, part in late:
        send_on(link, 0, 0, array, part)

    def sum_norms():
        total = norm_parts[0]
        for slot in range(1, cols * CORES):
            pltpu.make_async_copy(norm_parts.at[0], norm_parts.at[slot], near_recv.at[slot]).wait()
            total = total + norm_parts[slot]
        norm_slots[chip] = total

    def spread_norms():
        for n, (dz, dx) in enumerate(far):
            slot = (-dz % Z) * X + dx
            remote(
                norm_slots.at[chip], norm_slots.at[chip], norm_send.at[len(near) + n], far_recv.at[slot], far_id(dz, dx)
            )

    def came_in(sem, dz, dx, device_core, array, part):
        block = view(dz, dx, device_core, array, *PART[part])
        pltpu.make_async_copy(block, block, sem.at[place(dz, dx, array, part)]).wait()

    for n, (dz, dx, array, part, via) in enumerate(arrivals()):
        came_in(link_recv, dz, dx, core, array, part)
        for link in onward(dz, dx, array, part, via):
            send_on(link, dz, dx, array, part)
        hand_over(dz, dx, array, part)
        if n == 10:
            sum_norms()
        if n == 12:
            spread_norms()

    for dz, dx in far:
        slot = dz * X + dx
        there = lax.rem(z + dz, Z) * X + lax.rem(x + dx, X)
        pltpu.make_async_copy(norm_slots.at[there], norm_slots.at[there], far_recv.at[slot]).wait()
    for dz in range(Z):
        for dx in range(X):
            for array in range(4):
                for part in (RING_FIRST, ACROSS_FIRST):
                    if (dz, dx) != (0, 0) or array < 3:
                        came_in(core_recv, dz, dx, 1 - core, array, part)
    for copy in sends:
        copy.wait_send()


def store_kernel(query, key, value, mixed, slots, out_query, out_key, out_value, out_mixed, out_norm, sems):
    copies = []
    for source, target in ((query, out_query), (key, out_key), (value, out_value), (mixed, out_mixed)):
        rows = source.shape[0] // 4
        for k in range(4):
            part = pl.ds(k * rows, rows)
            copy = pltpu.make_async_copy(source.at[part, :], target.at[part, :], sems.at[len(copies)])
            copy.start()
            copies.append(copy)
    gains = jnp.concatenate([slots[k][:5] for k in range(CHIPS)], axis=0)
    out_norm[...] = gains.astype(jnp.bfloat16)
    for copy in copies:
        copy.wait()


def per_device(
    cols,
    weight_query, low_query, high_query,
    weight_key, low_key, high_key,
    weight_value, low_value, high_value,
    weight_mixed, low_mixed, high_mixed,
    norm_train, norm_step,
):
    tall, wide = (FULL, WIDTH), (WIDTH, FULL)
    piece = norm_train.shape[0]
    anywhere = pl.BlockSpec(memory_space=pl.ANY)
    in_vmem = pl.BlockSpec(memory_space=pltpu.VMEM)
    n_link = sum(len(onward(*u)) for u in arrivals()) + sum(len(s) for s in first_sends())
    n_core = len(arrivals()) + 6
    fulls = pl.pallas_call(
        functools.partial(gather_kernel, cols),
        name="gather",
        out_shape=[pltpu.VMEM(tall, jnp.bfloat16)] * 3
        + [pltpu.VMEM(wide, jnp.bfloat16), pltpu.VMEM((CHIPS, 8, 128), jnp.float32)],
        in_specs=[pl.BlockSpec(memory_space=pltpu.HBM)] * 14,
        out_specs=[in_vmem] * 5,
        scratch_shapes=[
            pltpu.VMEM((4, ROWS, WIDTH), jnp.bfloat16),
            pltpu.VMEM((4, RANK, ROWS), jnp.bfloat16),
            pltpu.VMEM((4, RANK, WIDTH), jnp.bfloat16),
            pltpu.VMEM((WIDTH, WIDTH), jnp.bfloat16),
            pltpu.VMEM((2, 1, piece), jnp.float32),
            pltpu.VMEM((cols * CORES, 8, 128), jnp.float32),
            pltpu.SemaphoreType.DMA((14,)),
            pltpu.SemaphoreType.DMA((n_link,)),
            pltpu.SemaphoreType.DMA((64,)),
            pltpu.SemaphoreType.DMA((n_core,)),
            pltpu.SemaphoreType.DMA((64,)),
            pltpu.SemaphoreType.DMA((2,)),
            pltpu.SemaphoreType.DMA((cols * CORES - 1 + CHIPS - 1,)),
            pltpu.SemaphoreType.DMA((cols * CORES,)),
            pltpu.SemaphoreType.DMA((CHIPS,)),
        ],
        compiler_params=pltpu.CompilerParams(
            collective_id=0, has_side_effects=True, vmem_limit_bytes=40_690_000
        ),
    )(
        weight_query, low_query.T, high_query,
        weight_key, low_key.T, high_key,
        weight_value, low_value.T, high_value,
        weight_mixed.T, low_mixed.T, high_mixed,
        norm_train.reshape(1, piece), norm_step.reshape(1, piece),
    )
    *ready, gains = pl.pallas_call(
        store_kernel,
        name="store",
        out_shape=[jax.ShapeDtypeStruct(tall, jnp.bfloat16)] * 3
        + [jax.ShapeDtypeStruct(wide, jnp.bfloat16), jax.ShapeDtypeStruct((CHIPS * 5, 128), jnp.bfloat16)],
        in_specs=[in_vmem] * 5,
        out_specs=[anywhere] * 4 + [in_vmem],
        scratch_shapes=[pltpu.SemaphoreType.DMA((16,))],
        compiler_params=pltpu.CompilerParams(vmem_limit_bytes=4 * 2**20),
    )(*fulls)
    return (*ready, gains.reshape(-1))


def solution(mesh):
    in_specs = (
        P("fsdp", "cols"),
        P("fsdp", None),
        P(None, "cols"),
        P("fsdp", "cols"),
        P("fsdp", None),
        P(None, "cols"),
        P("fsdp", "cols"),
        P("fsdp", None),
        P(None, "cols"),
        P("cols", "fsdp"),
        P("cols", None),
        P(None, "fsdp"),
        P(("fsdp", "cols")),
        P(("fsdp", "cols")),
    )
    out_specs = (P(None, "cols"), P(None, "cols"), P(None, "cols"), P("cols", None), P())
    return jax.shard_map(
        functools.partial(per_device, mesh.shape["cols"]),
        mesh=mesh,
        in_specs=in_specs,
        out_specs=out_specs,
        check_vma=False,
    )
```

time: 191 us -> 109 us (0.57)
  Pallas kernels: 0 us -> 108 us
  waiting for transfers between devices: 71.9 us -> 0 us
  blocking collectives: 68.9 us -> 0 us
  local copies, waits for them, and re-layouts: 28.6 us -> 0 us
  between operations: 14.1 us -> 0.65 us
  matrix products: 5.36 us -> 0 us
    pallas_call x0 -> x2, Pallas kernels: none -> 108 us  [the longest x1 98.9 us: per_device(): pl.pallas_call(functools.partial(gather_kernel, cols), name='gather', out...]
    all_gather x1 -> x0, waiting for transfers between devices: 71.9 us -> none  [rows_first(): result = lax.all_gather(both, axis, axis=0, tiled=True)]
    unnamed x1 -> x0, blocking collectives: 68.9 us -> none
    transpose x1 -> x0, local copies, waits for them, and re-layouts: 18.1 us -> none  [rows_first(): jnp.moveaxis(b.reshape(-1, *t.shape[1:]), 0, dim)]
    unnamed x9 -> x0, local copies, waits for them, and re-layouts: 10.5 us -> none
    dot_general x4 -> x0, matrix products: 5.36 us -> none  [the longest x1 1.37 us: per_device(): jnp.dot(low_mixed, high_mixed, preferred_element_type=jnp.float32)]
  transfers between devices with their start and end apart: 1 -> 0, of which waited for: 1 -> 0; matrix products, arithmetic and copies ran while one was open for 0% -> 0% of each run, Pallas kernels for 0% -> 0%
where the time goes in v1:
time: 109 us
  Pallas kernels  108 us (99%)
    pallas_call x1, Pallas kernels, per_device(): pl.pallas_call(functools.partial(gather_kernel, cols), name='gather', out...  98.9 us
    pallas_call x1, Pallas kernels, per_device(): pl.pallas_call(store_kernel, name='store', out_shape=[jax.ShapeDtypeStruc...  9.44 us

profile of v1, /device:TPU:1, one launch (start us, length us, event | category | flops | bytes accessed | tf_op | source)
XLA Modules:
  0.0 109.0 jit_solution(5662099814944478183)
XLA Ops:
  0.6 98.9 %gather.1 = (bf16[5120,640]{1,0:T(8,128)(2,1)S(1)}, bf16[5120,640]{1,0:T(8,128)(2,1)S(1)}, bf16[5120,640]{1,0:T(8,128)(2,1)S(1)}, bf16[640,5120]{1,0:T(8,128)(2,1)S(1)}, f32[8,8,128]{2,1,0:T(8,128)S(1)}) custom-call(bf16[320,640]{1,0:T(8,128)(2,1)} %weight_query.1, bf16[32,320]{1,0:T(8,128)(2,1)} %bitcast.10, bf16[32,640]{1,0:T(8,128)(2,1)} %high_query.1, ...), custom_call_target="tpu_custom_call" | custom-call | tf_op jit(solution)/shard_map/gather/pallas_call | solution.py:301
  99.5 9.4 %store.1 = (bf16[5120,640]{1,0:T(8,128)(2,1)}, bf16[5120,640]{1,0:T(8,128)(2,1)}, bf16[5120,640]{1,0:T(8,128)(2,1)}, bf16[640,5120]{1,0:T(8,128)(2,1)}, bf16[40,128]{1,0:T(8,128)(2,1)}) custom-call(bf16[5120,640]{1,0:T(8,128)(2,1)S(1)} %get-tuple-element.15.query, bf16[5120,640]{1,0:T(8,128)(2,1)S(1)} %get-tuple-element.16.key, ...), custom_call_target="tpu_custom_call" | custom-call | tf_op jit(solution)/shard_map/store/pallas_call | solution.py:335

commit v2 on v0

v2 whole, which is shorter than its diff:
```python
import functools
import heapq

import jax
import jax.numpy as jnp
from jax import lax
from jax.experimental import pallas as pl
from jax.experimental.pallas import tpu as pltpu
from jax.sharding import PartitionSpec as P

mix_rate = 2.0

Z, X, CORES = 4, 2, 2
CHIPS = Z * X
ROWS, WIDTH, RANK = 320, 640, 32
FULL = ROWS * CHIPS * CORES
RING_FIRST, ACROSS_FIRST = (0, 144), (144, 176)
RIGHT, LEFT, ACROSS = 0, 1, 2
LINKS = (RIGHT, LEFT, ACROSS)
QUERY, KEY, VALUE, MIXED = 0, 1, 2, 3


def own_sends(array):
    return [
        (ACROSS, 0, 0, array, 1, ACROSS_FIRST),
        (RIGHT, 0, 0, array, 1, RING_FIRST),
        (LEFT, 0, 0, array, 1, RING_FIRST),
    ]


def own_rest():
    sends = []
    for first, n in ((QUERY, 3), (MIXED, 1)):
        sends += [(ACROSS, 0, 0, first, n, RING_FIRST)]
        sends += [(RIGHT, 0, 0, first, n, ACROSS_FIRST), (LEFT, 0, 0, first, n, ACROSS_FIRST)]
    return sends


def forwards():
    sends = []
    for dz in (3, 1):
        for first, n in ((QUERY, 3), (MIXED, 1)):
            sends.append((ACROSS, dz, 0, first, n, RING_FIRST))
    for rows in (RING_FIRST, ACROSS_FIRST):
        sends.append((RIGHT, 3, 0, QUERY, 2, rows))
        sends += [(LEFT, 1, 0, VALUE, 1, rows), (LEFT, 1, 0, MIXED, 1, rows)]
    for first, n in ((QUERY, 3), (MIXED, 1)):
        sends += [(RIGHT, 0, 1, first, n, ACROSS_FIRST), (LEFT, 0, 1, first, n, ACROSS_FIRST)]
    sends += [(ACROSS, 2, 0, QUERY, 2, RING_FIRST), (ACROSS, 2, 0, VALUE, 1, RING_FIRST)]
    sends += [(ACROSS, 2, 0, MIXED, 1, (0, 112)), (ACROSS, 2, 0, MIXED, 1, (112, 32))]
    sends += [(RIGHT, 3, 1, QUERY, 2, (144, 128)), (RIGHT, 3, 1, QUERY, 2, (272, 48))]
    sends += [(LEFT, 1, 1, VALUE, 1, ACROSS_FIRST)]
    sends += [(LEFT, 1, 1, MIXED, 1, (144, 128)), (LEFT, 1, 1, MIXED, 1, (272, 48))]
    return sends


def seen_by_receiver(dz, dx, link):
    if link == RIGHT:
        return (dz - 1) % Z, dx
    if link == LEFT:
        return (dz + 1) % Z, dx
    return dz, 1 - dx


def cover(dz, dx, first, n, rows):
    way = RING_FIRST if rows[0] < ACROSS_FIRST[0] else ACROSS_FIRST
    return {(dz, dx, array, way) for array in range(first, first + n)}


def schedule():
    rate, gap, latency = 46.7e3, 0.1, 2.0
    sends, waiting = [], forwards()
    free, coming, here, order = [0.0] * 3, [], set(), []

    def issue(now, send):
        link, _, _, _, n, rows = send
        free[link] = max(free[link], now) + n * rows[1] * WIDTH * 2 / rate + gap
        heapq.heappush(coming, (free[link] + latency, len(sends)))
        sends.append(send)

    for array in range(4):
        for send in own_sends(array):
            issue(0.0, send)
    for send in own_rest():
        issue(0.0, send)
    while coming:
        now, number = heapq.heappop(coming)
        link, dz, dx, first, n, rows = sends[number]
        here |= cover(*seen_by_receiver(dz, dx, link), first, n, rows)
        ready = [send for send in waiting if cover(*send[1:]) <= here]
        waiting = [send for send in waiting if send not in ready]
        for send in ready:
            issue(now, send)
        order.append((now, number, len(ready)))
    assert not waiting
    return sends, order


def merge(weight, left, right):
    product = lax.dot_general(left, right, (((0,), (0,)), ((), ())), preferred_element_type=jnp.float32)
    return (weight.astype(jnp.float32) + mix_rate * product).astype(jnp.bfloat16)


def gather_kernel(
    cols,
    weight_query, low_query, high_query,
    weight_key, low_key, high_key,
    weight_value, low_value, high_value,
    weight_mixed, low_mixed, high_mixed,
    norm_train, norm_step,
    stack, mixed, norm_slots,
    weights, lefts, rights, mixed_pair, norms, norm_parts,
    in_sem, link_send, link_recv, core_send, core_recv, pair_sem, norm_send, norm_recv,
):
    f, c = lax.axis_index("fsdp"), lax.axis_index("cols")
    z, x, core = lax.div(f, X * CORES), lax.rem(lax.div(f, CORES), X), lax.rem(f, CORES)
    chip = lax.div(f, CORES)

    def at(device_z, device_x, device_core):
        return {"fsdp": device_z * (X * CORES) + device_x * CORES + device_core}

    neighbour = {
        RIGHT: at(lax.rem(z + 1, Z), x, core),
        LEFT: at(lax.rem(z + Z - 1, Z), x, core),
        ACROSS: at(z, 1 - x, core),
    }
    twin = at(z, x, 1 - core)
    up, down = {"cols": lax.rem(c + 2, cols)}, {"cols": lax.rem(c + cols - 2, cols)}
    over = {"cols": c + 1 - 2 * lax.rem(c, 2)}

    barrier = pltpu.get_barrier_semaphore()
    others = [(dz, dx) for dz in range(Z) for dx in range(X) if (dz, dx) != (0, 0)]
    others_at = [at(lax.rem(z + dz, Z), lax.rem(x + dx, X), core) for dz, dx in others]
    peers = [*others_at, twin, up, down, over]
    for peer in peers:
        pl.semaphore_signal(barrier, inc=1, device_id=peer, device_id_type=pl.DeviceIdType.MESH)

    inputs = (
        (weight_query, low_query, high_query),
        (weight_key, low_key, high_key),
        (weight_value, low_value, high_value),
        (weight_mixed, high_mixed, low_mixed),
    )
    loads = {}
    for k in (QUERY, KEY, MIXED, VALUE):
        targets = (weights.at[k], lefts.at[k], rights.at[k])
        loads[k] = [
            pltpu.make_async_copy(source, target, in_sem.at[3 * k + n])
            for n, (source, target) in enumerate(zip(inputs[k], targets))
        ]
    loads[4] = [
        pltpu.make_async_copy(source, norms.at[n], in_sem.at[12 + n]) for n, source in enumerate((norm_train, norm_step))
    ]
    for copies in loads.values():
        for copy in copies:
            copy.start()

    own_rows = pl.ds(pl.multiple_of(f * ROWS, 16), ROWS)
    own_half = pl.ds(pl.multiple_of(core * ROWS, 16), ROWS)

    def wait_loads(k):
        for copy in loads[k]:
            copy.wait()

    def merge_own(k):
        wait_loads(k)
        merged = merge(weights[k], lefts[k], rights[k])
        if k == MIXED:
            mixed_pair[own_half, :] = merged
        else:
            stack[k, own_rows, :] = merged

    started = []

    def remote(source, target, send_sem, recv_sem, device):
        copy = pltpu.make_async_remote_copy(
            src_ref=source,
            dst_ref=target,
            send_sem=send_sem,
            recv_sem=recv_sem,
            device_id=device,
            device_id_type=pl.DeviceIdType.MESH,
        )
        copy.start()
        started.append(copy)

    def view(dz, dx, device_core, first, n, rows):
        block = lax.rem(z + dz, Z) * X + lax.rem(x + dx, X)
        start, many = rows
        if first == MIXED:
            start = pl.multiple_of(device_core * ROWS + start, 16)
            return mixed.at[pl.ds(start, many), pl.ds(pl.multiple_of(block * WIDTH, 128), WIDTH)]
        start = pl.multiple_of((block * CORES + device_core) * ROWS + start, 16)
        return stack.at[pl.ds(first, n), pl.ds(start, many), :]

    sends, order = schedule()
    issued = []

    def send_next():
        number = len(issued)
        link, *what = sends[number]
        issued.append(number)
        block = view(what[0], what[1], core, *what[2:])
        remote(block, block, link_send.at[number], link_recv.at[number], neighbour[link])

    def hand_over(number, *what):
        block = view(what[0], what[1], core, *what[2:])
        remote(block, block, core_send.at[number], core_recv.at[number], twin)

    def landed(sem, number, device_core, *what):
        block = view(what[0], what[1], device_core, *what[2:])
        pltpu.make_async_copy(block, block, sem.at[number]).wait()

    def norm_copy(number, source, target, device):
        remote(source, target, norm_send.at[number], norm_recv.at[number], device)

    def norm_wait(number, buffer):
        pltpu.make_async_copy(buffer, buffer, norm_recv.at[number]).wait()

    mine, twins, chips_sum, below, above, beyond, line_sum, overs = (norm_parts.at[k] for k in range(8))

    def norm_start():
        wait_loads(4)
        piece = norms.shape[-1]
        gain = (norms[0] + norms[1]).astype(jnp.bfloat16)
        gain = jnp.broadcast_to(gain.astype(jnp.float32), (8, piece)).astype(jnp.bfloat16)
        offset = (core * cols + c) * piece
        lane = lax.broadcasted_iota(jnp.int32, (piece, 128), 1)
        element = lax.broadcasted_iota(jnp.int32, (piece, 128), 0)
        row = lax.broadcasted_iota(jnp.int32, (8, 128), 0)
        tile = jnp.zeros((8, 128), jnp.float32)
        for r in range(5):
            hot = jnp.where(lane + 128 * r == element + offset, 1.0, 0.0).astype(jnp.bfloat16)
            spread = jnp.dot(gain, hot, preferred_element_type=jnp.float32)
            tile = jnp.where(row == r, spread, tile)
        mine[chip] = tile

    def norm_to_group():
        for (dz, dx), device in zip(others, others_at):
            norm_copy((-dz % Z) * X + dx, mine.at[chip], mine.at[chip], device)

    def norm_to_twin():
        for dz, dx in others:
            there = lax.rem(z + dz, Z) * X + lax.rem(x + dx, X)
            norm_wait(dz * X + dx, mine.at[there])
        norm_copy(8, mine, twins, twin)

    def norm_add_twin():
        norm_wait(8, twins)
        chips_sum[...] = mine[...] + twins[...]

    def norm_to_line():
        norm_copy(9, chips_sum, below, up)
        norm_copy(10, chips_sum, above, down)

    def norm_along_line():
        norm_wait(9, below)
        norm_copy(11, below, beyond, up)
        norm_wait(10, above)

    def norm_add_line():
        norm_wait(11, beyond)
        line_sum[...] = chips_sum[...] + below[...] + above[...] + beyond[...]

    def norm_over():
        norm_copy(12, line_sum, overs, over)

    def norm_end():
        norm_wait(12, overs)
        norm_slots[...] = line_sum[...] + overs[...]

    norm_steps = [
        (16, norm_to_twin), (21, norm_add_twin), (24, norm_to_line), (30, norm_along_line),
        (36, norm_add_line), (39, norm_over), (76, norm_end),
    ]

    own = [(len(sends), 0, 0, QUERY, 2, (0, ROWS)), (len(sends) + 1, 0, 0, VALUE, 1, (0, ROWS))]
    merge_own(QUERY)
    merge_own(KEY)
    pl.semaphore_wait(barrier, len(peers))
    for _ in own_sends(QUERY):
        send_next()
    norm_start()
    merge_own(MIXED)
    norm_to_group()
    for _ in own_sends(KEY):
        send_next()
    merge_own(VALUE)
    half = mixed_pair.at[own_half, :]
    remote(half, half, pair_sem.at[0], pair_sem.at[1], twin)
    pair = started[-1]
    hand_over(*own[0])

    pair.wait_recv()
    turned = mixed_pair[...].astype(jnp.float32).T.astype(jnp.bfloat16)
    mixed[:, pl.ds(pl.multiple_of(chip * WIDTH, 128), WIDTH)] = turned
    for _ in own_sends(VALUE):
        send_next()
    hand_over(*own[1])
    for _ in own_sends(MIXED) + own_rest():
        send_next()

    for now, number, ready in order:
        link, dz, dx, *what = sends[number]
        dz, dx = seen_by_receiver(dz, dx, link)
        landed(link_recv, number, core, dz, dx, *what)
        for _ in range(ready):
            send_next()
        hand_over(number, dz, dx, *what)
        if norm_steps and now >= norm_steps[0][0]:
            norm_steps.pop(0)[1]()
    assert not norm_steps

    for number, dz, dx, *what in own:
        landed(core_recv, number, 1 - core, dz, dx, *what)
    for _, number, _ in order:
        link, dz, dx, *what = sends[number]
        dz, dx = seen_by_receiver(dz, dx, link)
        landed(core_recv, number, 1 - core, dz, dx, *what)
    for copy in started:
        copy.wait_send()


def store_kernel(stack, mixed, slots, out_query, out_key, out_value, out_mixed, out_norm, gains, sems):
    copies = []

    def store(source, target):
        copy = pltpu.make_async_copy(source, target, sems.at[len(copies)])
        copy.start()
        copies.append(copy)

    for k, target in enumerate((out_query, out_key, out_value)):
        for part in range(4):
            rows = pl.ds(part * (FULL // 4), FULL // 4)
            store(stack.at[k, rows, :], target.at[rows, :])
    for part in range(4):
        rows = pl.ds(part * (WIDTH // 4), WIDTH // 4)
        store(mixed.at[rows, :], out_mixed.at[rows, :])
    tiles = [slots[chip][:5] for chip in range(CHIPS)]
    gains[...] = jnp.concatenate(tiles, axis=0).astype(jnp.bfloat16)
    store(gains, out_norm)
    for copy in copies:
        copy.wait()


def per_device(
    cols,
    weight_query, low_query, high_query,
    weight_key, low_key, high_key,
    weight_value, low_value, high_value,
    weight_mixed, low_mixed, high_mixed,
    norm_train, norm_step,
):
    tall, wide = (FULL, WIDTH), (WIDTH, FULL)
    piece = norm_train.shape[0]
    anywhere = pl.BlockSpec(memory_space=pl.ANY)
    in_vmem = pl.BlockSpec(memory_space=pltpu.VMEM)
    n_link = len(schedule()[0])
    gathered = pl.pallas_call(
        functools.partial(gather_kernel, cols),
        name="gather",
        out_shape=[
            pltpu.VMEM((3, *tall), jnp.bfloat16),
            pltpu.VMEM(wide, jnp.bfloat16),
            pltpu.VMEM((CHIPS, 8, 128), jnp.float32),
        ],
        in_specs=[pl.BlockSpec(memory_space=pltpu.HBM)] * 14,
        out_specs=[in_vmem] * 3,
        scratch_shapes=[
            pltpu.VMEM((4, ROWS, WIDTH), jnp.bfloat16),
            pltpu.VMEM((4, RANK, ROWS), jnp.bfloat16),
            pltpu.VMEM((4, RANK, WIDTH), jnp.bfloat16),
            pltpu.VMEM((WIDTH, WIDTH), jnp.bfloat16),
            pltpu.VMEM((2, 1, piece), jnp.float32),
            pltpu.VMEM((8, CHIPS, 8, 128), jnp.float32),
            pltpu.SemaphoreType.DMA((14,)),
            pltpu.SemaphoreType.DMA((n_link,)),
            pltpu.SemaphoreType.DMA((n_link,)),
            pltpu.SemaphoreType.DMA((n_link + 2,)),
            pltpu.SemaphoreType.DMA((n_link + 2,)),
            pltpu.SemaphoreType.DMA((2,)),
            pltpu.SemaphoreType.DMA((13,)),
            pltpu.SemaphoreType.DMA((13,)),
        ],
        compiler_params=pltpu.CompilerParams(
            collective_id=0, has_side_effects=True, vmem_limit_bytes=40_690_000
        ),
    )(
        weight_query, low_query.T, high_query,
        weight_key, low_key.T, high_key,
        weight_value, low_value.T, high_value,
        weight_mixed.T, low_mixed.T, high_mixed,
        norm_train.reshape(1, piece), norm_step.reshape(1, piece),
    )
    *ready, gains = pl.pallas_call(
        store_kernel,
        name="store",
        out_shape=[jax.ShapeDtypeStruct(tall, jnp.bfloat16)] * 3
        + [jax.ShapeDtypeStruct(wide, jnp.bfloat16), jax.ShapeDtypeStruct((CHIPS * 5, 128), jnp.bfloat16)],
        in_specs=[in_vmem] * 3,
        out_specs=[anywhere] * 5,
        scratch_shapes=[pltpu.VMEM((CHIPS * 5, 128), jnp.bfloat16), pltpu.SemaphoreType.DMA((17,))],
        compiler_params=pltpu.CompilerParams(vmem_limit_bytes=4 * 2**20),
    )(*gathered)
    return (*ready, gains.reshape(-1))


def solution(mesh):
    in_specs = (
        P("fsdp", "cols"),
        P("fsdp", None),
        P(None, "cols"),
        P("fsdp", "cols"),
        P("fsdp", None),
        P(None, "cols"),
        P("fsdp", "cols"),
        P("fsdp", None),
        P(None, "cols"),
        P("cols", "fsdp"),
        P("cols", None),
        P(None, "fsdp"),
        P(("fsdp", "cols")),
        P(("fsdp", "cols")),
    )
    out_specs = (P(None, "cols"), P(None, "cols"), P(None, "cols"), P("cols", None), P())
    return jax.shard_map(
        functools.partial(per_device, mesh.shape["cols"]),
        mesh=mesh,
        in_specs=in_specs,
        out_specs=out_specs,
        check_vma=False,
    )
```

time: 191 us -> 104 us (0.54)
  Pallas kernels: 0 us -> 103 us
  waiting for transfers between devices: 71.9 us -> 0 us
  blocking collectives: 68.9 us -> 0 us
  local copies, waits for them, and re-layouts: 28.6 us -> 0 us
  between operations: 14.1 us -> 0.65 us
  matrix products: 5.36 us -> 0 us
    pallas_call x0 -> x2, Pallas kernels: none -> 103 us  [the longest x1 94.3 us: per_device(): pl.pallas_call(functools.partial(gather_kernel, cols), name='gather', out...]
    all_gather x1 -> x0, waiting for transfers between devices: 71.9 us -> none  [rows_first(): result = lax.all_gather(both, axis, axis=0, tiled=True)]
    unnamed x1 -> x0, blocking collectives: 68.9 us -> none
    transpose x1 -> x0, local copies, waits for them, and re-layouts: 18.1 us -> none  [rows_first(): jnp.moveaxis(b.reshape(-1, *t.shape[1:]), 0, dim)]
    unnamed x9 -> x0, local copies, waits for them, and re-layouts: 10.5 us -> none
    dot_general x4 -> x0, matrix products: 5.36 us -> none  [the longest x1 1.37 us: per_device(): jnp.dot(low_mixed, high_mixed, preferred_element_type=jnp.float32)]
  transfers between devices with their start and end apart: 1 -> 0, of which waited for: 1 -> 0; matrix products, arithmetic and copies ran while one was open for 0% -> 0% of each run, Pallas kernels for 0% -> 0%
where the time goes in v2:
time: 104 us
  Pallas kernels  103 us (99%)
    pallas_call x1, Pallas kernels, per_device(): pl.pallas_call(functools.partial(gather_kernel, cols), name='gather', out...  94.3 us
    pallas_call x1, Pallas kernels, per_device(): pl.pallas_call(store_kernel, name='store', out_shape=[jax.ShapeDtypeStruc...  8.85 us

profile of v2, /device:TPU:1, one launch (start us, length us, event | category | flops | bytes accessed | tf_op | source)
XLA Modules:
  0.0 103.8 jit_solution(505834127222817250)
XLA Ops:
  0.6 94.3 %gather.1 = (bf16[3,5120,640]{2,1,0:T(8,128)(2,1)S(1)}, bf16[640,5120]{1,0:T(8,128)(2,1)S(1)}, f32[8,8,128]{2,1,0:T(8,128)S(1)}) custom-call(bf16[320,640]{1,0:T(8,128)(2,1)} %weight_query.1, bf16[32,320]{1,0:T(8,128)(2,1)} %bitcast.10, bf16[32,640]{1,0:T(8,128)(2,1)} %high_query.1, bf16[320,640]{1,0:T(8,128)(2,1)} %weight_key.1, bf16[32,320]{1,0:T(8,128)(2,1)} %bitcast.11, ...), custom_call_target="tpu_custom_call" | custom-call | tf_op jit(solution)/shard_map/gather/pallas_call | solution.py:359
  95.0 8.9 %store.1 = (bf16[5120,640]{1,0:T(8,128)(2,1)}, bf16[5120,640]{1,0:T(8,128)(2,1)}, bf16[5120,640]{1,0:T(8,128)(2,1)}, bf16[640,5120]{1,0:T(8,128)(2,1)}, bf16[40,128]{1,0:T(8,128)(2,1)}) custom-call(bf16[3,5120,640]{2,1,0:T(8,128)(2,1)S(1)} %get-tuple-element.13.stack, bf16[640,5120]{1,0:T(8,128)(2,1)S(1)} %get-tuple-element.14.mixed, ...), custom_call_target="tpu_custom_call" | custom-call | tf_op jit(solution)/shard_map/store/pallas_call | solution.py:395
